TPU v7x, 32 devices: a whole 2x2x4 slice. The times are simulated.
32 devices in a mesh: ya: 8 (over z, y), zb: 4 (over x, core).
Axes of the slice: x: 2, y: 2, z: 4, core: 2. Of those that a mesh axis runs over, the one named last changes fastest.
Arguments:
- source: float32 [128, 128, 512], P(None, 'ya', 'zb'), may hold values from -6 to 6
- symbol_x: float32 [128], replicated, may hold values from 0.3 to 3
- symbol_y: float32 [128], replicated, may hold values from 0.3 to 3
- symbol_z: float32 [512], replicated, may hold values from 0.3 to 3
Outputs:
- modes: float32 [128, 128, 512], P('ya', 'zb')
All inputs are finite; a program needn't handle non-finite values.
Results may differ from a plain program's by a relative error of at most 0.000071.
Values sent between devices are 32-bit elements; how exact they have to be, the bound alone decides.
A program may use at most 64 MiB of HBM per device.

v0:
```python
import functools

import jax
import jax.numpy as jnp
import numpy as np
from jax import lax
from jax.experimental import pallas as pl
from jax.experimental.pallas import tpu as pltpu
from jax.sharding import PartitionSpec as P

MESH = pl.DeviceIdType.MESH
AHEAD = 2
SHARES = (5,5,4,2)


def transform_table(count):
    rank = np.arange(1, count + 1)
    angle = np.pi / (count + 1) * (rank[:, None] * rank[None, :] % (2 * count + 2))
    table = np.sqrt(2.0 / (count + 1)) * np.sin(angle)
    high = table.astype(jnp.bfloat16)
    low = (table - high.astype(np.float64)).astype(jnp.bfloat16)
    return high, low


def halves(values):
    high = values.astype(jnp.bfloat16)
    return high, (values - high.astype(jnp.float32)).astype(jnp.bfloat16)


def left_product(table3, values):
    high, low = halves(values)
    stacked = jnp.concatenate([high, low, high], axis=0)
    return jnp.dot(table3, stacked, preferred_element_type=jnp.float32)


def partners(me, count):
    if count & (count - 1):
        return (
            [lax.rem(me + step, count) for step in range(count)],
            [lax.rem(me + count - step, count) for step in range(count)],
        )
    peers, bit = [me], 1
    while bit < count:
        turn = bit * (1 - 2 * lax.rem(lax.div(me, bit), 2))
        peers += [peer + turn for peer in peers]
        bit *= 2
    return peers, peers


def kernel(
    n_ya, n_zb, bounds,
    source, table_x, table_y, high_z, low_z, symbol_x, symbol_y, symbol_z,
    out,
    src, tx, ty, hz, lz, sx, sy, sz, first, second, third, lines, column_x, base,
    load_sem, met, send_a, recv_a, send_b, recv_b,
):
    ya, zb = lax.axis_index("ya"), lax.axis_index("zb")
    nx, yl, zl = source.shape
    ny = yl * n_ya
    kl = nx // n_ya
    jl = ny // n_zb
    nz = zl * n_zb
    chunks = len(bounds) - 1

    barrier = pltpu.get_barrier_semaphore()

    to_a, from_a = partners(ya, n_ya)
    to_b, from_b = partners(zb, n_zb)
    paired = n_ya & (n_ya - 1) == 0
    direct = [step for step in range(1, n_ya) if not paired or step & (step - 1) == 0]
    rounds = len(direct) - 1 if paired else 0
    greeted = [("ya", to_a[step]) for step in reversed(direct)] + [("zb", peer) for peer in to_b[1:]]
    for axis, peer in greeted:
        pl.semaphore_signal(barrier, inc=1, device_id={axis: peer}, device_id_type=MESH)

    loads = [
        pltpu.make_async_copy(a, b, load_sem.at[i])
        for i, (a, b) in enumerate(
            [
                (source, src), (table_x, tx), (table_y, ty), (high_z, hz), (low_z, lz),
                (symbol_x, sx), (symbol_y, sy), (symbol_z, sz),
            ]
        )
    ]
    for load in loads:
        load.start()

    loads[0].wait()
    loads[1].wait()

    def tell(turn):
        if turn < rounds:
            pl.semaphore_signal(
                met.at[turn], inc=1, device_id={"ya": to_a[2**turn]}, device_id_type=MESH
            )

    flat_src = src.reshape(nx * yl, zl)
    flat_first = first.reshape(nx * yl, zl)

    def x_step(pair, _):
        values = jnp.concatenate(
            [flat_src[pl.ds(2 * pair + t, nx, stride=yl), :] for t in range(2)], axis=1
        )
        modes = left_product(tx[...], values)
        for t in range(2):
            flat_first[pl.ds(2 * pair + t, nx, stride=yl), :] = modes[:, t * zl:(t + 1) * zl]
        return 0

    lax.fori_loop(0, yl // 2, x_step, 0, unroll=8)

    pl.semaphore_wait(barrier, len(greeted))
    tell(0)

    def size(chunk):
        return bounds[chunk + 1] - bounds[chunk]

    def span(chunk):
        return pl.ds(bounds[chunk], size(chunk))

    def copy_a(chunk, step):
        peer = to_a[step]
        return pltpu.make_async_remote_copy(
            src_ref=first.at[pl.ds(peer * kl + bounds[chunk], size(chunk))],
            dst_ref=second.at[span(chunk), pl.ds(pl.multiple_of(ya * yl, yl), yl)],
            send_sem=send_a.at[chunk, step],
            recv_sem=recv_a.at[chunk, step],
            device_id={"ya": peer},
            device_id_type=MESH,
        )

    def arrive_a(chunk, step):
        peer = from_a[step]
        there = second.at[span(chunk), pl.ds(pl.multiple_of(peer * yl, yl), yl)]
        return pltpu.make_async_copy(there, there, recv_a.at[chunk, step])

    def copy_b(chunk, step):
        peer = to_b[step]
        return pltpu.make_async_remote_copy(
            src_ref=third.at[span(chunk), pl.ds(pl.multiple_of(peer * jl, jl), jl)],
            dst_ref=lines.at[zb, span(chunk)],
            send_sem=send_b.at[chunk, step],
            recv_sem=recv_b.at[chunk, step],
            device_id={"zb": peer},
            device_id_type=MESH,
        )

    def arrive_b(chunk, step):
        there = lines.at[from_b[step], span(chunk)]
        return pltpu.make_async_copy(there, there, recv_b.at[chunk, step])

    order = [*range(n_ya // 2, n_ya), *range(n_ya // 2 - 1, 0, -1)]

    def each_a(todo):
        for step in order:
            todo(step)

    def each_b(todo):
        for step in range(n_zb - 1, 0, -1):
            todo(step)

    heard = 0
    for step in order:
        need = (step - 2 ** (step.bit_length() - 1)).bit_length() if paired else 0
        while heard < need:
            pl.semaphore_wait(met.at[heard], 1)
            heard += 1
            tell(heard)
        copy_a(0, step).start()
    while heard < rounds:
        pl.semaphore_wait(met.at[heard], 1)
        heard += 1
        tell(heard)
    for chunk in range(1, min(AHEAD, chunks)):
        each_a(lambda step: copy_a(chunk, step).start())

    second[:, pl.ds(pl.multiple_of(ya * yl, yl), yl), :] = first[pl.ds(ya * kl, kl)]

    for load in loads[2:]:
        load.wait()

    def column(row):
        return jnp.broadcast_to(row, (zl, row.shape[1])).T

    column_x[...] = column(sx[...])
    third[0] = column(sy[...])
    own_y = third[0, pl.ds(pl.multiple_of(zb * jl, jl), jl), :]
    base[...] = jnp.concatenate([own_y] * n_zb, axis=1) + sz[...]

    def y_stage(chunk):
        each_a(lambda step: arrive_a(chunk, step).wait())
        if chunk + AHEAD < chunks:
            each_a(lambda step: copy_a(chunk + AHEAD, step).start())
        for low in range(bounds[chunk], bounds[chunk + 1], 2):
            planes = range(low, min(low + 2, bounds[chunk + 1]))
            values = jnp.concatenate([second[k] for k in planes], axis=1)
            modes = left_product(ty[...], values)
            for t, k in enumerate(planes):
                third[k] = modes[:, t * zl:(t + 1) * zl]
        each_b(lambda step: copy_b(chunk, step).start())
        lines[zb, span(chunk)] = third[
            span(chunk), pl.ds(pl.multiple_of(zb * jl, jl), jl), :
        ]

    def z_stage(chunk):
        each_b(lambda step: arrive_b(chunk, step).wait())
        values = jnp.concatenate(
            [lines[b, span(chunk)].reshape(size(chunk) * jl, zl) for b in range(n_zb)], axis=1
        )
        high, low = halves(values)
        dot = functools.partial(jnp.dot, preferred_element_type=jnp.float32)
        both = dot(jnp.concatenate([high, low], axis=0), hz[...])
        rows = high.shape[0]
        modes = both[:rows] + both[rows:] + dot(high, lz[...])
        for t in range(size(chunk)):
            k = bounds[chunk] + t
            own_x = jnp.concatenate([column_x[pl.ds(ya * kl + k, 1), :]] * n_zb, axis=1)
            out[k] = modes[t * jl:(t + 1) * jl] * lax.rsqrt(base[...] + own_x)

    for chunk in range(chunks):
        y_stage(chunk)
        if chunk:
            z_stage(chunk - 1)
    z_stage(chunks - 1)

    for chunk in range(chunks):
        each_a(lambda step: copy_a(chunk, step).wait_send())
        each_b(lambda step: copy_b(chunk, step).wait_send())


def body(n_ya, n_zb, source, symbol_x, symbol_y, symbol_z):
    nx, yl, zl = source.shape
    ny, nz = yl * n_ya, zl * n_zb
    kl, jl = nx // n_ya, ny // n_zb
    ends = np.cumsum(SHARES) * kl // sum(SHARES)
    bounds = tuple(sorted({0, *ends.tolist()}))
    chunks = len(bounds) - 1
    tables = []
    for count in (nx, ny):
        high, low = transform_table(count)
        tables.append(np.concatenate([high, high, low], axis=1))
    tables += list(transform_table(nz))
    room = 67_043_328 - 4 * kl * jl * nz - 2**18
    dma = pltpu.SemaphoreType.DMA
    vmem = pltpu.VMEM
    return pl.pallas_call(
        functools.partial(kernel, n_ya, n_zb, bounds),
        out_shape=pltpu.VMEM((kl, jl, nz), jnp.float32),
        in_specs=[pl.BlockSpec(memory_space=pltpu.HBM)] * 8,
        out_specs=pl.BlockSpec(memory_space=pltpu.VMEM),
        scratch_shapes=[
            vmem((nx, yl, zl), jnp.float32),
            vmem((nx, 3 * nx), jnp.bfloat16),
            vmem((ny, 3 * ny), jnp.bfloat16),
            vmem((nz, nz), jnp.bfloat16),
            vmem((nz, nz), jnp.bfloat16),
            vmem((1, nx), jnp.float32),
            vmem((1, ny), jnp.float32),
            vmem((1, nz), jnp.float32),
            vmem((nx, yl, zl), jnp.float32),
            vmem((kl, ny, zl), jnp.float32),
            vmem((kl, ny, zl), jnp.float32),
            vmem((n_zb, kl, jl, zl), jnp.float32),
            vmem((nx, zl), jnp.float32),
            vmem((jl, nz), jnp.float32),
            dma((8,)),
            pltpu.SemaphoreType.REGULAR((max(1, n_ya.bit_length() - 2),)),
            dma((chunks, n_ya)),
            dma((chunks, n_ya)),
            dma((chunks, n_zb)),
            dma((chunks, n_zb)),
        ],
        compiler_params=pltpu.CompilerParams(
            collective_id=0, has_side_effects=True, vmem_limit_bytes=room
        ),
    )(
        source, *[jnp.asarray(t) for t in tables],
        symbol_x[None], symbol_y[None], symbol_z[None],
    )


def solution(mesh):
    placed = (P(None, "ya", "zb"), P(), P(), P())
    return jax.shard_map(
        functools.partial(body, mesh.shape["ya"], mesh.shape["zb"]),
        mesh=mesh, in_specs=placed, out_specs=P("ya", "zb", None), check_vma=False,
    )
```

profile of v0, /device:TPU:0, one launch (start us, length us, event | category | flops | bytes accessed | tf_op | source)
XLA Modules:
  0.0 36.4 jit_solution(13159165996548093813)
XLA Ops:
  0.0 35.4 %shard_map.82 = f32[16,32,512]{2,1,0:T(8,128)S(1)} custom-call(f32[128,16,128]{2,1,0:T(8,128)} %source.1, bf16[128,384]{1,0:T(8,128)(2,1)} %constant.6.clone.table_x.table_y, bf16[128,384]{1,0:T(8,128)(2,1)} %constant.6.clone.table_x.table_y, bf16[512,512]{1,0:T(8,128)(2,1)} %constant.7.clone.high_z, bf16[512,512]{1,0:T(8,128)(2,1)} %constant.8.clone.low_z, ...), custom_call_target="tpu_custom_call" | custom-call | tf_op jit(solution)/shard_map/pallas_call | solution.py:245
  35.4 1.0 %copy.10 = f32[16,32,512]{2,1,0:T(8,128)} copy(f32[16,32,512]{2,1,0:T(8,128)S(1)} %shard_map.82) | data formatting | bytes 2097152
where the time goes:
time: 36.5 us; the launch traced here: 36.4 us
  Pallas kernels  35.4 us (97%)
  local copies, waits for them, and re-layouts  0.97 us (3%)
    pallas_call x1, Pallas kernels, body(): pl.pallas_call(functools.partial(kernel, n_ya, n_zb, bounds), out_shape=p...  35.4 us
    unnamed x1, local copies, waits for them, and re-layouts  0.97 us

commit v1 on v0

v1 whole, which is shorter than its diff:
```python
import functools

import jax
import jax.numpy as jnp
import numpy as np
from jax import lax
from jax.experimental import pallas as pl
from jax.experimental.pallas import tpu as pltpu
from jax.sharding import PartitionSpec as P

MESH = pl.DeviceIdType.MESH
SHARES = (3, 3, 2, 2, 2, 2, 2)
LAG = 3
LEAD = 2
EARLY = 2
CUT = 4


def transform_table(count):
    rank = np.arange(1, count + 1)
    angle = np.pi / (count + 1) * (rank[:, None] * rank[None, :] % (2 * count + 2))
    table = np.sqrt(2.0 / (count + 1)) * np.sin(angle)
    high = table.astype(jnp.bfloat16)
    low = (table - high.astype(np.float64)).astype(jnp.bfloat16)
    return high, low


def halves(values):
    high = values.astype(jnp.bfloat16)
    return high, (values - high.astype(jnp.float32)).astype(jnp.bfloat16)


def left_product(table3, values):
    high, low = halves(values)
    stacked = jnp.concatenate([high, low, high], axis=0)
    return jnp.dot(table3, stacked, preferred_element_type=jnp.float32)


def partners(me, count):
    if count & (count - 1):
        return [lax.rem(me + step, count) for step in range(count)]
    peers, bit = [me], 1
    while bit < count:
        turn = bit * (1 - 2 * lax.rem(lax.div(me, bit), 2))
        peers += [peer + turn for peer in peers]
        bit *= 2
    return peers


def kernel(
    n_ya, n_zb, bounds,
    source, table_x, table_y, table_z, symbol_x, symbol_y, symbol_z,
    out,
    src, tx, ty, tz, sx, sy, sz, first, second, third, lines, column_x, base,
    load_sem, here_a, here_b, send_a, recv_a, send_b, recv_b,
):
    ya, zb = lax.axis_index("ya"), lax.axis_index("zb")
    nx, yl, zl = source.shape
    ny = yl * n_ya
    kl = nx // n_ya
    jl = ny // n_zb
    chunks = len(bounds) - 1
    cut = CUT if yl % CUT == 0 else yl
    to_a, to_b = partners(ya, n_ya), partners(zb, n_zb)

    barrier = pltpu.get_barrier_semaphore()

    def greet(axis, me, count):
        def one(peer, _):
            pl.semaphore_signal(barrier, inc=1, device_id={axis: peer}, device_id_type=MESH)
            return 0

        lax.fori_loop(me + 1, count, one, 0)

    greet("ya", ya, n_ya)
    greet("zb", zb, n_zb)

    rows = [pl.ds(low, cut) for low in range(0, yl, cut)]
    pairs = [(source.at[:, row], src.at[:, row]) for row in rows] + [
        (table_x, tx), (table_y, ty), (table_z, tz),
        (symbol_x, sx), (symbol_y, sy), (symbol_z, sz),
    ]
    loads = [pltpu.make_async_copy(a, b, load_sem.at[i]) for i, (a, b) in enumerate(pairs)]
    parts = len(rows)
    loads[parts].start()
    for load in loads[:parts]:
        load.start()

    flat_src = src.reshape(nx * yl, zl)
    flat_first = first.reshape(nx * yl, zl)

    def x_step(pair, _):
        values = jnp.concatenate(
            [flat_src[pl.ds(2 * pair + t, nx, stride=yl), :] for t in range(2)], axis=1
        )
        modes = left_product(tx[...], values)
        for t in range(2):
            flat_first[pl.ds(2 * pair + t, nx, stride=yl), :] = modes[:, t * zl:(t + 1) * zl]
        return 0

    def size(chunk):
        return bounds[chunk + 1] - bounds[chunk]

    def span(chunk):
        return pl.ds(bounds[chunk], size(chunk))

    def copy_a(chunk, peer, low, count):
        return pltpu.make_async_remote_copy(
            src_ref=first.at[pl.ds(peer * kl + bounds[chunk], size(chunk)), pl.ds(low, count)],
            dst_ref=second.at[
                span(chunk), pl.ds(pl.multiple_of(ya * yl + low, cut), count)
            ],
            send_sem=send_a,
            recv_sem=recv_a.at[chunk],
            device_id={"ya": peer},
            device_id_type=MESH,
        )

    order = [*range(n_ya // 2, n_ya), *range(n_ya // 2 - 1, 0, -1)]

    def each_a(todo, lower):
        for step in order:
            peer = to_a[step]
            pl.when(peer < ya if lower else peer > ya)(functools.partial(todo, peer))

    def copy_b(chunk, step):
        peer = to_b[step]
        return pltpu.make_async_remote_copy(
            src_ref=third.at[span(chunk), pl.ds(pl.multiple_of(peer * jl, jl), jl)],
            dst_ref=lines.at[zb, span(chunk)],
            send_sem=send_b,
            recv_sem=recv_b.at[chunk],
            device_id={"zb": peer},
            device_id_type=MESH,
        )

    def all_of(ref, sem):
        return pltpu.make_async_copy(ref, ref, sem)

    pl.when(ya + zb > 0)(lambda: pl.semaphore_wait(barrier, ya + zb))

    def answer(peer, _):
        pl.semaphore_signal(here_a.at[ya], inc=1, device_id={"ya": peer}, device_id_type=MESH)
        return 0

    def answer_b(peer, _):
        pl.semaphore_signal(here_b, inc=1, device_id={"zb": peer}, device_id_type=MESH)
        return 0

    lax.fori_loop(0, ya, answer, 0)
    lax.fori_loop(0, zb, answer_b, 0)

    for part in range(parts):
        if part == 0:
            loads[parts].wait()
            loads[part].wait()
            for load in loads[parts + 1:]:
                load.start()
        else:
            loads[part].wait()
        lax.fori_loop(part * cut // 2, (part + 1) * cut // 2, x_step, 0, unroll=True)
        each_a(lambda peer: copy_a(0, peer, part * cut, cut).start(), True)

    def serve(chunk, peer):
        copy_a(chunk, peer, 0, yl).start()

    for chunk in range(1, min(LEAD + 1, chunks)):
        pl.when(ya > 0)(functools.partial(serve, chunk, 0))
    for chunk in range(1, chunks):
        if chunk + LEAD < chunks:
            pl.when(ya > 0)(functools.partial(serve, chunk + LEAD, 0))
        each_a(lambda peer: pl.when(peer > 0)(functools.partial(serve, chunk, peer)), True)

    for peer in range(1, n_ya):
        @pl.when(peer > ya)
        def _():
            pl.semaphore_wait(here_a.at[peer], 1)
            for part in range(parts):
                copy_a(0, peer, part * cut, cut).start()
            for chunk in range(1, min(EARLY, chunks)):
                serve(chunk, peer)
    for chunk in range(EARLY, chunks):
        each_a(functools.partial(serve, chunk), False)

    second[:, pl.ds(pl.multiple_of(ya * yl, yl), yl), :] = first[pl.ds(ya * kl, kl)]

    for load in loads[parts + 1:]:
        load.wait()

    def column(row):
        return jnp.broadcast_to(row, (zl, row.shape[1])).T

    column_x[...] = column(sx[...])
    third[0] = column(sy[...])
    own_y = third[0, pl.ds(pl.multiple_of(zb * jl, jl), jl), :]
    base[...] = jnp.concatenate([own_y] * n_zb, axis=1) + sz[...]
    above = n_zb - 1 - zb
    pl.when(above > 0)(lambda: pl.semaphore_wait(here_b, above))

    def y_stage(chunk):
        all_of(second.at[span(chunk), pl.ds(0, ny - yl)], recv_a.at[chunk]).wait()
        for low in range(bounds[chunk], bounds[chunk + 1], 2):
            planes = range(low, min(low + 2, bounds[chunk + 1]))
            values = jnp.concatenate([second[k] for k in planes], axis=1)
            modes = left_product(ty[...], values)
            for t, k in enumerate(planes):
                third[k] = modes[:, t * zl:(t + 1) * zl]
        for step in range(n_zb - 1, 0, -1):
            copy_b(chunk, step).start()
        lines[zb, span(chunk)] = third[
            span(chunk), pl.ds(pl.multiple_of(zb * jl, jl), jl), :
        ]

    def z_stage(chunk):
        all_of(third.at[span(chunk), pl.ds(0, ny - jl)], recv_b.at[chunk]).wait()
        values = jnp.concatenate(
            [lines[b, span(chunk)].reshape(size(chunk) * jl, zl) for b in range(n_zb)], axis=1
        )
        high, low = halves(values)
        dot = functools.partial(jnp.dot, preferred_element_type=jnp.float32)
        both = dot(jnp.concatenate([high, low], axis=0), tz[0])
        rows = high.shape[0]
        modes = both[:rows] + both[rows:] + dot(high, tz[1])
        for t in range(size(chunk)):
            k = bounds[chunk] + t
            own_x = jnp.concatenate([column_x[pl.ds(ya * kl + k, 1), :]] * n_zb, axis=1)
            out[k] = modes[t * jl:(t + 1) * jl] * lax.rsqrt(base[...] + own_x)

    for turn in range(chunks + LAG):
        if turn < chunks:
            y_stage(turn)
        if turn >= LAG:
            z_stage(turn - LAG)

    all_of(first.at[pl.ds(0, nx - kl)], send_a).wait()
    all_of(third.at[:, pl.ds(0, ny - jl)], send_b).wait()


def body(n_ya, n_zb, source, symbol_x, symbol_y, symbol_z):
    nx, yl, zl = source.shape
    ny, nz = yl * n_ya, zl * n_zb
    kl, jl = nx // n_ya, ny // n_zb
    ends = np.cumsum(SHARES) * kl // sum(SHARES)
    bounds = tuple(sorted({0, *ends.tolist()}))
    chunks = len(bounds) - 1
    tables = []
    for count in (nx, ny):
        high, low = transform_table(count)
        tables.append(np.concatenate([high, high, low], axis=1))
    tables.append(np.stack(transform_table(nz)))
    room = 67_043_328 - 4 * kl * jl * nz - 2**18
    dma = pltpu.SemaphoreType.DMA
    regular = pltpu.SemaphoreType.REGULAR
    vmem = pltpu.VMEM
    return pl.pallas_call(
        functools.partial(kernel, n_ya, n_zb, bounds),
        out_shape=pltpu.VMEM((kl, jl, nz), jnp.float32),
        in_specs=[pl.BlockSpec(memory_space=pltpu.HBM)] * 7,
        out_specs=pl.BlockSpec(memory_space=pltpu.VMEM),
        scratch_shapes=[
            vmem((nx, yl, zl), jnp.float32),
            vmem((nx, 3 * nx), jnp.bfloat16),
            vmem((ny, 3 * ny), jnp.bfloat16),
            vmem((2, nz, nz), jnp.bfloat16),
            vmem((1, nx), jnp.float32),
            vmem((1, ny), jnp.float32),
            vmem((1, nz), jnp.float32),
            vmem((nx, yl, zl), jnp.float32),
            vmem((kl, ny, zl), jnp.float32),
            vmem((kl, ny, zl), jnp.float32),
            vmem((n_zb, kl, jl, zl), jnp.float32),
            vmem((nx, zl), jnp.float32),
            vmem((jl, nz), jnp.float32),
            dma((6 + (yl // CUT if yl % CUT == 0 else 1),)),
            regular((n_ya,)),
            regular,
            dma,
            dma((chunks,)),
            dma,
            dma((chunks,)),
        ],
        compiler_params=pltpu.CompilerParams(
            collective_id=0, has_side_effects=True, vmem_limit_bytes=room
        ),
    )(
        source, *[jnp.asarray(t) for t in tables],
        symbol_x[None], symbol_y[None], symbol_z[None],
    )


def solution(mesh):
    placed = (P(None, "ya", "zb"), P(), P(), P())
    return jax.shard_map(
        functools.partial(body, mesh.shape["ya"], mesh.shape["zb"]),
        mesh=mesh, in_specs=placed, out_specs=P("ya", "zb", None), check_vma=False,
    )
```

time: 36.5 us -> 33.7 us (0.923)
  the two profiles are of different devices: /device:TPU:0 before, /device:TPU:4 now
where the time goes in v1:
time: 33.7 us; the launch traced here: 33.1 us
  Pallas kernels  32.1 us (95%)
  local copies, waits for them, and re-layouts  0.97 us (3%)
    pallas_call x1, Pallas kernels, body(): pl.pallas_call(functools.partial(kernel, n_ya, n_zb, bounds), out_shape=p...  32.1 us
    unnamed x1, local copies, waits for them, and re-layouts  0.97 us

profile of v1, /device:TPU:4, one launch (start us, length us, event | category | flops | bytes accessed | tf_op | source)
XLA Modules:
  0.0 33.1 jit_solution(1034051619189914547)
XLA Ops:
  0.0 32.1 %shard_map.73 = f32[16,32,512]{2,1,0:T(8,128)S(1)} custom-call(f32[128,16,128]{2,1,0:T(8,128)} %source.1, bf16[128,384]{1,0:T(8,128)(2,1)} %constant.4.clone.table_x.table_y, bf16[128,384]{1,0:T(8,128)(2,1)} %constant.4.clone.table_x.table_y, bf16[2,512,512]{2,1,0:T(8,128)(2,1)} %constant.5.clone.table_z, f32[1,128]{1,0:T(1,128)} %bitcast.4, ...), custom_call_target="tpu_custom_call" | custom-call | tf_op jit(solution)/shard_map/pallas_call | solution.py:255
  32.1 1.0 %copy.9 = f32[16,32,512]{2,1,0:T(8,128)} copy(f32[16,32,512]{2,1,0:T(8,128)S(1)} %shard_map.73) | data formatting | bytes 2097152

commit v2 on v1

v2 whole, which is shorter than its diff:
```python
import functools
import math

import jax
import jax.numpy as jnp
import numpy as np
from jax import lax
from jax.experimental import pallas as pl
from jax.experimental.pallas import tpu as pltpu
from jax.sharding import PartitionSpec as P

MESH = pl.DeviceIdType.MESH
SHARES = (3, 3, 2, 2, 2, 2, 2)
LAG = 3
PIECES = 4
LEAD = 2
LATE = 3
BEHIND = 2
DIRECT = 2
CUTS = (2, 8)
BARPOS = 0
EARLY = 3
BEYOND = (2, 4, 6)


def transform_table(count):
    rank = np.arange(1, count + 1)
    angle = np.pi / (count + 1) * (rank[:, None] * rank[None, :] % (2 * count + 2))
    table = np.sqrt(2.0 / (count + 1)) * np.sin(angle)
    high = table.astype(jnp.bfloat16)
    low = (table - high.astype(np.float64)).astype(jnp.bfloat16)
    return high, low


def halves(values):
    high = values.astype(jnp.bfloat16)
    return high, (values - high.astype(jnp.float32)).astype(jnp.bfloat16)


def left_product(table3, values):
    high, low = halves(values)
    stacked = jnp.concatenate([high, low, high], axis=0)
    return jnp.dot(table3, stacked, preferred_element_type=jnp.float32)


def right_product(lines, planes, table):
    parts = [lines[b, planes] for b in range(lines.shape[0])]
    rows = parts[0].shape[0] * parts[0].shape[1]
    values = jnp.concatenate([part.reshape(rows, part.shape[2]) for part in parts], axis=1)
    high, low = halves(values)
    dot = functools.partial(jnp.dot, preferred_element_type=jnp.float32)
    both = dot(jnp.concatenate([high, low], axis=0), table[0])
    return both[:rows] + both[rows:] + dot(high, table[1])


def partners(me, count):
    if count & (count - 1):
        return [lax.rem(me + step, count) for step in range(count)]
    peers, bit = [me], 1
    while bit < count:
        turn = bit * (1 - 2 * lax.rem(lax.div(me, bit), 2))
        peers += [peer + turn for peer in peers]
        bit *= 2
    return peers


def kernel(
    n_ya, n_zb, bounds,
    source, table_x, table_y, table_z, symbol_x, symbol_y, symbol_z,
    out, last, scale, tz,
    src, tx, ty, sx, sy, sz, first, second, third, lines, relay, column_x, base,
    local_sem, here_a, here_b, recv_a, recv_r, recv_b,
):
    ya, zb = lax.axis_index("ya"), lax.axis_index("zb")
    nx, yl, zl = source.shape
    ny = yl * n_ya
    kl = nx // n_ya
    jl = ny // n_zb
    chunks = len(bounds) - 1
    cuts = [0, *(c for c in CUTS if c < yl), yl]
    to_a, to_b = partners(ya, n_ya), partners(zb, n_zb)

    half, quarter = n_ya // 2, 0 if n_ya & (n_ya - 1) else n_ya // 4
    cross = [step ^ (quarter > 1) for step in range(half, n_ya)]
    aside = [*range(half - 1, 0, -1)]
    if not quarter:
        cross, aside = [*range(1, n_ya)], []
    lower_end, upper_end = ya < quarter, ya >= n_ya - quarter
    at_end = lower_end | upper_end
    inner = jnp.logical_not(at_end)
    nearby = to_a[quarter]

    barrier = pltpu.get_barrier_semaphore()

    def greet(axis, low, high):
        def one(peer, _):
            pl.semaphore_signal(barrier, inc=1, device_id={axis: peer}, device_id_type=MESH)
            return 0

        lax.fori_loop(low, high, one, 0)

    greet("ya", ya + 1, n_ya)
    greet("zb", zb + 1, n_zb)

    parts = len(cuts) - 1
    rows = [pl.ds(low, high - low) for low, high in zip(cuts, cuts[1:])]
    loads = [
        pltpu.make_async_copy(source.at[:, row], src.at[:, row], local_sem.at[i])
        for i, row in enumerate(rows)
    ]
    table = pltpu.make_async_copy(table_x, tx, local_sem.at[parts])
    send_a, send_r, send_b = [local_sem.at[i] for i in (parts + 1, 0, parts)]
    late = [
        pltpu.make_async_copy(a, b, local_sem.at[parts if i == 0 else i - 1 if i <= parts else i + 1])
        for i, (a, b) in enumerate(
            [(table_y, ty), (table_z, tz), (symbol_x, sx), (symbol_y, sy), (symbol_z, sz)]
        )
    ]
    table.start()
    for load in loads:
        load.start()

    flat_src = src.reshape(nx * yl, zl)
    flat_first = first.reshape(nx * yl, zl)

    def x_step(pair, _):
        values = jnp.concatenate(
            [flat_src[pl.ds(2 * pair + t, nx, stride=yl), :] for t in range(2)], axis=1
        )
        modes = left_product(tx[...], values)
        for t in range(2):
            flat_first[pl.ds(2 * pair + t, nx, stride=yl), :] = modes[:, t * zl:(t + 1) * zl]
        return 0

    def size(chunk):
        return bounds[chunk + 1] - bounds[chunk]

    def span(chunk):
        return pl.ds(bounds[chunk], size(chunk))

    def rows_of(peer, low, count):
        return pl.ds(pl.multiple_of(peer * yl + low, math.gcd(yl, low)), count)

    def copy_a(chunk, peer, low=0, count=yl):
        return pltpu.make_async_remote_copy(
            src_ref=first.at[peer, span(chunk), pl.ds(low, count)],
            dst_ref=second.at[span(chunk), rows_of(ya, low, count)],
            send_sem=send_a,
            recv_sem=recv_a.at[chunk],
            device_id={"ya": peer},
            device_id_type=MESH,
        )

    def hand_over(chunk, low=0, count=yl):
        other = jnp.where(ya < half, half, 0)
        return pltpu.make_async_remote_copy(
            src_ref=first.at[pl.ds(other, half), span(chunk), pl.ds(low, count)],
            dst_ref=relay.at[:, span(chunk), pl.ds(low, count)],
            send_sem=send_a,
            recv_sem=recv_r.at[chunk],
            device_id={"ya": nearby},
            device_id_type=MESH,
        )

    def pass_on(chunk, step):
        peer = to_a[step]
        return pltpu.make_async_remote_copy(
            src_ref=relay.at[lax.rem(peer, half), span(chunk)],
            dst_ref=second.at[span(chunk), rows_of(nearby, 0, yl)],
            send_sem=send_r,
            recv_sem=recv_a.at[chunk],
            device_id={"ya": peer},
            device_id_type=MESH,
        )

    def each_a(todo, lower, steps):
        for step in steps:
            peer = to_a[step]
            pl.when(peer < ya if lower else peer > ya)(functools.partial(todo, peer))

    def serve(chunk, peer, low=0, count=yl):
        copy_a(chunk, peer, low, count).start()

    def copy_b(chunk, step):
        peer = to_b[step]
        return pltpu.make_async_remote_copy(
            src_ref=third.at[span(chunk), pl.ds(pl.multiple_of(peer * jl, jl), jl)],
            dst_ref=last.at[zb] if chunk == chunks - 1 else lines.at[zb, span(chunk)],
            send_sem=send_b,
            recv_sem=recv_b.at[chunk],
            device_id={"zb": peer},
            device_id_type=MESH,
        )

    def all_of(ref, sem):
        return pltpu.make_async_copy(ref, ref, sem)

    def meet():
        below = ya + zb
        pl.when(below > 0)(lambda: pl.semaphore_wait(barrier, below))

        def answer(peer, _):
            pl.semaphore_signal(
                here_a.at[ya - 1], inc=1, device_id={"ya": peer}, device_id_type=MESH
            )
            return 0

        def answer_b(peer, _):
            pl.semaphore_signal(here_b, inc=1, device_id={"zb": peer}, device_id_type=MESH)
            return 0

        lax.fori_loop(jnp.where(ya < half, 0, quarter), ya, answer, 0)
        lax.fori_loop(0, zb, answer_b, 0)

    if BARPOS == 0:
        meet()
    for part in range(parts):
        low, count = cuts[part], cuts[part + 1] - cuts[part]
        if part == 0:
            table.wait()
            loads[0].wait()
            for i, load in enumerate(late):
                if i < 2 or i > parts:
                    load.start()
        else:
            loads[part].wait()
            if 2 <= part + 1 < len(late):
                late[part + 1].start()
        if part == 0 and BARPOS == 1:
            meet()
        lax.fori_loop(low // 2, (low + count) // 2, x_step, 0, unroll=True)
        if part == 0 and BARPOS == 2:
            meet()
        if quarter and not DIRECT:
            pl.when(upper_end)(lambda: hand_over(0, low, count).start())
        pl.when(inner | (upper_end & (DIRECT > 0)))(
            lambda: each_a(lambda peer: serve(0, peer, low, count), True, cross)
        )
        each_a(lambda peer: serve(0, peer, low, count), True, aside)

    near = [step for step in aside if step >= quarter] if quarter else []
    own = [step for step in aside if step not in near]

    if quarter:
        @pl.when(upper_end)
        def _():
            for turn in range(1, chunks + BEHIND):
                if turn < DIRECT:
                    each_a(functools.partial(serve, turn), True, cross)
                elif turn < chunks:
                    hand_over(turn).start()
                if turn < chunks:
                    each_a(functools.partial(serve, turn), True, own)
                if turn > BEHIND:
                    each_a(functools.partial(serve, turn - BEHIND), True, near)

        @pl.when(lower_end)
        def _():
            for chunk in range(1, chunks):
                each_a(functools.partial(serve, chunk), True, own)

    @pl.when(inner)
    def _():
        for chunk in range(1, chunks):
            if chunk < EARLY:
                each_a(functools.partial(serve, chunk), True, cross)
            each_a(functools.partial(serve, chunk), True, aside)

    for peer in range(1, n_ya):
        reached = peer > ya
        if quarter and peer >= half:
            reached &= jnp.logical_not(lower_end)

        @pl.when(reached)
        def _():
            pl.semaphore_wait(here_a.at[peer - 1], 1)
            if quarter:
                pl.when(lower_end & (nearby == peer))(lambda: hand_over(0).start())
            for chunk in range(min(EARLY, chunks)):
                serve(chunk, peer)

    if quarter:
        @pl.when(lower_end)
        def _():
            for turn in range(1, chunks + BEHIND):
                if turn < chunks:
                    hand_over(turn).start()
                if turn < chunks and turn >= EARLY:
                    each_a(functools.partial(serve, turn), False, own)
                if turn - BEHIND >= EARLY:
                    each_a(functools.partial(serve, turn - BEHIND), False, near)

        @pl.when(upper_end)
        def _():
            for chunk in range(EARLY, chunks):
                each_a(functools.partial(serve, chunk), False, own)

    @pl.when(inner)
    def _():
        for chunk in range(EARLY, chunks):
            each_a(functools.partial(serve, chunk), False, aside)

    second[:, pl.ds(pl.multiple_of(ya * yl, yl), yl), :] = first[ya]

    for load in late:
        load.wait()

    def column(row):
        return jnp.broadcast_to(row, (zl, row.shape[1])).T

    column_x[...] = column(sx[...])
    third[0] = column(sy[...])
    own_y = third[0, pl.ds(pl.multiple_of(zb * jl, jl), jl), :]
    base[...] = jnp.concatenate([own_y] * n_zb, axis=1) + sz[...]
    above = n_zb - 1 - zb
    pl.when(above > 0)(lambda: pl.semaphore_wait(here_b, above))

    def y_stage(chunk):
        all_of(second.at[span(chunk), pl.ds(0, ny - yl)], recv_a.at[chunk]).wait()
        for low in range(bounds[chunk], bounds[chunk + 1], 2):
            planes = range(low, min(low + 2, bounds[chunk + 1]))
            values = jnp.concatenate([second[k] for k in planes], axis=1)
            modes = left_product(ty[...], values)
            for t, k in enumerate(planes):
                third[k] = modes[:, t * zl:(t + 1) * zl]
        for step in range(n_zb - 1, 0, -1):
            copy_b(chunk, step).start()
        mine = third[span(chunk), pl.ds(pl.multiple_of(zb * jl, jl), jl), :]
        if chunk == chunks - 1:
            last[zb] = mine
        else:
            lines[zb, span(chunk)] = mine

    def scale_of(k):
        own_x = jnp.concatenate([column_x[pl.ds(ya * kl + k, 1), :]] * n_zb, axis=1)
        return lax.rsqrt(base[...] + own_x)

    for t in range(size(chunks - 1)):
        scale[t] = scale_of(bounds[-2] + t)

    def z_stage(chunk):
        all_of(third.at[span(chunk), pl.ds(0, ny - jl)], recv_b.at[chunk]).wait()
        if chunk == chunks - 1:
            return
        modes = right_product(lines, span(chunk), tz)
        for t in range(size(chunk)):
            k = bounds[chunk] + t
            out[k] = modes[t * jl:(t + 1) * jl] * scale_of(k)

    def push(turn):
        if quarter:
            got = all_of(relay.at[:, span(turn)], recv_r.at[turn])

            @pl.when(ya < half)
            def _():
                got.wait()
                for step in cross:
                    pass_on(turn, step).start()

            if turn >= DIRECT:
                @pl.when(ya >= half)
                def _():
                    got.wait()
                    for step in cross:
                        pl.when(to_a[step] == 0)(lambda: pass_on(turn, step).start())
                    rest = [
                        c for c in range(DIRECT, chunks)
                        if min(c + LEAD * (c >= LATE), chunks - 1) == turn
                    ]
                    for late in rest:
                        for step in cross:
                            pl.when(to_a[step] > 0)(lambda: pass_on(late, step).start())

        if turn + EARLY < chunks:
            for step in cross:
                serve(turn + EARLY, to_a[step])

    pushed = 0
    for turn in range(chunks + LAG):
        upto = min(chunks, 1 + BEYOND[turn] if turn < len(BEYOND) else chunks)
        if pushed < upto:
            @pl.when(inner)
            def _():
                for early in range(pushed, upto):
                    push(early)
            pushed = upto
        if turn < chunks:
            y_stage(turn)
        if turn >= LAG:
            z_stage(turn - LAG)

    all_of(first.at[pl.ds(0, n_ya - 1)], send_a).wait()
    if quarter:
        pl.when(inner & (ya < half))(lambda: all_of(relay, send_r).wait())
        later = relay.at[:, pl.ds(bounds[DIRECT], kl - bounds[DIRECT])]
        pl.when(inner & (ya >= half))(lambda: all_of(later, send_r).wait())
    all_of(third.at[:, pl.ds(0, ny - jl)], send_b).wait()


def finish(done, last, scale, table, out, final, sems):
    planes, rows = scale.shape[0], scale.shape[1]
    ready = done.shape[0] - planes
    cuts = [ready * piece // PIECES for piece in range(PIECES + 1)]
    copies = [
        pltpu.make_async_copy(done.at[low:high], out.at[low:high], sems.at[i])
        for i, (low, high) in enumerate(zip(cuts, cuts[1:]))
    ]
    for copy in copies:
        copy.start()
    modes = right_product(last, slice(None), table)
    for t in range(planes):
        final[t] = modes[t * rows:(t + 1) * rows] * scale[t]
        copies.append(pltpu.make_async_copy(final.at[t], out.at[ready + t], sems.at[PIECES + t]))
        copies[-1].start()
    for copy in copies:
        copy.wait()


def body(n_ya, n_zb, source, symbol_x, symbol_y, symbol_z):
    nx, yl, zl = source.shape
    ny, nz = yl * n_ya, zl * n_zb
    kl, jl = nx // n_ya, ny // n_zb
    ends = np.cumsum(SHARES) * kl // sum(SHARES)
    bounds = tuple(sorted({0, *ends.tolist()}))
    chunks = len(bounds) - 1
    tables = []
    for count in (nx, ny):
        high, low = transform_table(count)
        tables.append(np.concatenate([high, high, low], axis=1))
    tables.append(np.stack(transform_table(nz)))
    final = kl - bounds[-2]
    shapes = [(kl, jl, nz), (n_zb, final, jl, zl), (final, jl, nz)]
    room = 67_043_328 - 4 * sum(int(np.prod(shape)) for shape in shapes) - 4 * nz * nz - 2**18
    outs = [pltpu.VMEM(shape, jnp.float32) for shape in shapes]
    outs.append(pltpu.VMEM((2, nz, nz), jnp.bfloat16))
    dma = pltpu.SemaphoreType.DMA
    regular = pltpu.SemaphoreType.REGULAR
    vmem = pltpu.VMEM
    ready = pl.pallas_call(
        functools.partial(kernel, n_ya, n_zb, bounds),
        out_shape=outs,
        in_specs=[pl.BlockSpec(memory_space=pltpu.HBM)] * 7,
        out_specs=[pl.BlockSpec(memory_space=pltpu.VMEM)] * 4,
        scratch_shapes=[
            vmem((nx, yl, zl), jnp.float32),
            vmem((nx, 3 * nx), jnp.bfloat16),
            vmem((ny, 3 * ny), jnp.bfloat16),
            vmem((1, nx), jnp.float32),
            vmem((1, ny), jnp.float32),
            vmem((1, nz), jnp.float32),
            vmem((n_ya, kl, yl, zl), jnp.float32),
            vmem((kl, ny, zl), jnp.float32),
            vmem((kl, ny, zl), jnp.float32),
            vmem((n_zb, kl, jl, zl), jnp.float32),
            vmem((max(1, n_ya // 2), kl, yl, zl), jnp.float32),
            vmem((nx, zl), jnp.float32),
            vmem((jl, nz), jnp.float32),
            dma((2 + max(1 + sum(c < yl for c in CUTS), 4),)),
            regular((max(1, n_ya - 1),)),
            regular,
            dma((chunks,)),
            dma((chunks,)),
            dma((chunks,)),
        ],
        compiler_params=pltpu.CompilerParams(
            collective_id=0, has_side_effects=True, vmem_limit_bytes=room
        ),
    )(
        source, *[jnp.asarray(t) for t in tables],
        symbol_x[None], symbol_y[None], symbol_z[None],
    )
    return pl.pallas_call(
        finish,
        out_shape=jax.ShapeDtypeStruct((kl, jl, nz), jnp.float32),
        in_specs=[pl.BlockSpec(memory_space=pltpu.VMEM)] * 4,
        out_specs=pl.BlockSpec(memory_space=pltpu.HBM),
        scratch_shapes=[vmem((final, jl, nz), jnp.float32), dma((PIECES + final,))],
        compiler_params=pltpu.CompilerParams(vmem_limit_bytes=2**24),
    )(*[pltpu.with_memory_space_constraint(r, pltpu.VMEM) for r in ready])


def solution(mesh):
    placed = (P(None, "ya", "zb"), P(), P(), P())
    return jax.shard_map(
        functools.partial(body, mesh.shape["ya"], mesh.shape["zb"]),
        mesh=mesh, in_specs=placed, out_specs=P("ya", "zb", None), check_vma=False,
    )
```

time: 33.7 us -> 33 us (0.979); the launches traced: 33.1 us -> 32.8 us
  local copies, waits for them, and re-layouts: 0.97 us -> 0 us
  Pallas kernels: 32.1 us -> 32.8 us
    unnamed x1 -> x0, local copies, waits for them, and re-layouts: 0.97 us -> none
    pallas_call x1 -> x2, Pallas kernels: 32.1 us -> 32.8 us  [the longest x1 31.8 us: body(): pl.pallas_call(functools.partial(kernel, n_ya, n_zb, bounds), out_shape=o...]
where the time goes in v2:
time: 33 us; the launch traced here: 32.8 us
  Pallas kernels  32.8 us (99%)
    pallas_call x1, Pallas kernels, body(): pl.pallas_call(functools.partial(kernel, n_ya, n_zb, bounds), out_shape=o...  31.8 us
    pallas_call x1, Pallas kernels, body(): pl.pallas_call(finish, out_shape=jax.ShapeDtypeStruct((kl, jl, nz), jnp.f...  1.02 us

profile of v2, /device:TPU:4, one launch (start us, length us, event | category | flops | bytes accessed | tf_op | source)
XLA Modules:
  0.0 32.8 jit_solution(5274041647591515412)
XLA Ops:
  0.0 31.8 %shard_map.73 = (f32[16,32,512]{2,1,0:T(8,128)S(1)}, f32[4,2,32,128]{3,2,1,0:T(8,128)S(1)}, f32[2,32,512]{2,1,0:T(8,128)S(1)}, bf16[2,512,512]{2,1,0:T(8,128)(2,1)S(1)}) custom-call(f32[128,16,128]{2,1,0:T(8,128)} %source.1, bf16[128,384]{1,0:T(8,128)(2,1)} %constant.4.clone.table_x.table_y, bf16[128,384]{1,0:T(8,128)(2,1)} %constant.4.clone.table_x.table_y, ...), custom_call_target="tpu_custom_call" | custom-call | tf_op jit(solution)/shard_map/pallas_call | solution.py:439
  31.8 1.0 %shard_map.74 = f32[16,32,512]{2,1,0:T(8,128)} custom-call(f32[16,32,512]{2,1,0:T(8,128)S(1)} %get-tuple-element.9.done, f32[4,2,32,128]{3,2,1,0:T(8,128)S(1)} %get-tuple-element.10.last, f32[2,32,512]{2,1,0:T(8,128)S(1)} %get-tuple-element.11.scale, bf16[2,512,512]{2,1,0:T(8,128)(2,1)S(1)} %get-tuple-element.12.table), custom_call_target="tpu_custom_call" | custom-call | tf_op jit(solution)/shard_map/pallas_call | solution.py:472

commit v3 on v2

--- a/solution.py
+++ b/solution.py
@@ -13,13 +13,16 @@
 SHARES = (3, 3, 2, 2, 2, 2, 2)
 LAG = 3
 PIECES = 4
-LEAD = 2
-LATE = 3
+LEAD = 1
+LATE = 2
 BEHIND = 2
 DIRECT = 2
 CUTS = (2, 8)
 BARPOS = 0
 EARLY = 3
+OFF = 1
+SPLIT = 5
+SHIFT = 0
 BEYOND = (2, 4, 6)
 
 
@@ -348,32 +351,51 @@
             out[k] = modes[t * jl:(t + 1) * jl] * scale_of(k)
 
     def push(turn):
-        if quarter:
-            got = all_of(relay.at[:, span(turn)], recv_r.at[turn])
-
-            @pl.when(ya < half)
-            def _():
+        own_due = turn + OFF if EARLY <= turn + OFF < chunks else None
+
+        def own(chunk, wanted):
+            for step in cross:
+                peer = to_a[step]
+                pl.when(wanted(peer))(functools.partial(serve, chunk, peer))
+
+        def passed(chunk, wanted):
+            for step in cross:
+                pl.when(wanted(to_a[step]))(lambda: pass_on(chunk, step).start())
+
+        def anyone(peer):
+            return peer >= 0
+
+        def first_one(peer):
+            return peer == 0
+
+        def the_rest(peer):
+            return peer > 0
+
+        got = all_of(relay.at[:, span(turn)], recv_r.at[turn]) if quarter else None
+
+        @pl.when(ya < half)
+        def _():
+            if quarter:
                 got.wait()
-                for step in cross:
-                    pass_on(turn, step).start()
-
-            if turn >= DIRECT:
-                @pl.when(ya >= half)
-                def _():
-                    got.wait()
-                    for step in cross:
-                        pl.when(to_a[step] == 0)(lambda: pass_on(turn, step).start())
-                    rest = [
-                        c for c in range(DIRECT, chunks)
-                        if min(c + LEAD * (c >= LATE), chunks - 1) == turn
-                    ]
-                    for late in rest:
-                        for step in cross:
-                            pl.when(to_a[step] > 0)(lambda: pass_on(late, step).start())
-
-        if turn + EARLY < chunks:
-            for step in cross:
-                serve(turn + EARLY, to_a[step])
+                passed(turn, anyone)
+            if own_due is not None:
+                own(own_due, anyone)
+
+        @pl.when(ya >= half)
+        def _():
+            if quarter and turn >= DIRECT:
+                got.wait()
+                passed(turn, first_one)
+            if own_due is not None:
+                own(own_due, first_one)
+            rest = [(c, True) for c in range(EARLY, chunks) if c >= SPLIT and c == turn + SHIFT]
+            if own_due is not None and own_due < SPLIT:
+                rest.append((own_due, True))
+            for c in range(DIRECT, chunks) if quarter else ():
+                if min(c + LEAD * (c >= LATE), chunks - 1) == turn:
+                    rest.append((c, False))
+            for c, mine in rest:
+                (own if mine else passed)(c, the_rest)
 
     pushed = 0
     for turn in range(chunks + LAG):

time: 33 us -> 32.6 us (0.988)
  Pallas kernels: 32.8 us -> 32.4 us
    pallas_call x1, Pallas kernels: 31.8 us -> 31.4 us  [body(): pl.pallas_call(functools.partial(kernel, n_ya, n_zb, bounds), out_shape=o...]
where the time goes in v3:
time: 32.6 us; the launch traced here: 32.4 us
  Pallas kernels  32.4 us (99%)
    pallas_call x1, Pallas kernels, body(): pl.pallas_call(functools.partial(kernel, n_ya, n_zb, bounds), out_shape=o...  31.4 us
    pallas_call x1, Pallas kernels, body(): pl.pallas_call(finish, out_shape=jax.ShapeDtypeStruct((kl, jl, nz), jnp.f...  1.02 us

profile of v3, /device:TPU:4, one launch (start us, length us, event | category | flops | bytes accessed | tf_op | source)
XLA Modules:
  0.0 32.4 jit_solution(4017533575055515618)
XLA Ops:
  0.0 31.4 %shard_map.73 = (f32[16,32,512]{2,1,0:T(8,128)S(1)}, f32[4,2,32,128]{3,2,1,0:T(8,128)S(1)}, f32[2,32,512]{2,1,0:T(8,128)S(1)}, bf16[2,512,512]{2,1,0:T(8,128)(2,1)S(1)}) custom-call(f32[128,16,128]{2,1,0:T(8,128)} %source.1, bf16[128,384]{1,0:T(8,128)(2,1)} %constant.4.clone.table_x.table_y, bf16[128,384]{1,0:T(8,128)(2,1)} %constant.4.clone.table_x.table_y, ...), custom_call_target="tpu_custom_call" | custom-call | tf_op jit(solution)/shard_map/pallas_call | solution.py:461
  31.4 1.0 %shard_map.74 = f32[16,32,512]{2,1,0:T(8,128)} custom-call(f32[16,32,512]{2,1,0:T(8,128)S(1)} %get-tuple-element.9.done, f32[4,2,32,128]{3,2,1,0:T(8,128)S(1)} %get-tuple-element.10.last, f32[2,32,512]{2,1,0:T(8,128)S(1)} %get-tuple-element.11.scale, bf16[2,512,512]{2,1,0:T(8,128)(2,1)S(1)} %get-tuple-element.12.table), custom_call_target="tpu_custom_call" | custom-call | tf_op jit(solution)/shard_map/pallas_call | solution.py:494

commit v4 on v3

--- a/solution.py
+++ b/solution.py
@@ -10,20 +10,18 @@
 from jax.sharding import PartitionSpec as P
 
 MESH = pl.DeviceIdType.MESH
-SHARES = (3, 3, 2, 2, 2, 2, 2)
+SHARES = (3, 3, 3, 3, 2, 1, 1)
 LAG = 3
 PIECES = 4
 LEAD = 1
-LATE = 2
 BEHIND = 2
 DIRECT = 2
 CUTS = (2, 8)
-BARPOS = 0
 EARLY = 3
 OFF = 1
 SPLIT = 5
-SHIFT = 0
-BEYOND = (2, 4, 6)
+TAIL = 3
+BEYOND = (2, 4, 5, 6)
 
 
 def transform_table(count):
@@ -215,8 +213,8 @@
         lax.fori_loop(jnp.where(ya < half, 0, quarter), ya, answer, 0)
         lax.fori_loop(0, zb, answer_b, 0)
 
-    if BARPOS == 0:
-        meet()
+    even = lax.rem(ya, 2) == 0
+    pl.when(jnp.logical_not(even))(meet)
     for part in range(parts):
         low, count = cuts[part], cuts[part + 1] - cuts[part]
         if part == 0:
@@ -229,11 +227,9 @@
             loads[part].wait()
             if 2 <= part + 1 < len(late):
                 late[part + 1].start()
-        if part == 0 and BARPOS == 1:
-            meet()
         lax.fori_loop(low // 2, (low + count) // 2, x_step, 0, unroll=True)
-        if part == 0 and BARPOS == 2:
-            meet()
+        if part == 0:
+            pl.when(even)(meet)
         if quarter and not DIRECT:
             pl.when(upper_end)(lambda: hand_over(0, low, count).start())
         pl.when(inner | (upper_end & (DIRECT > 0)))(
@@ -350,6 +346,13 @@
             k = bounds[chunk] + t
             out[k] = modes[t * jl:(t + 1) * jl] * scale_of(k)
 
+    def later(chunk, start, offset):
+        if chunk >= chunks - TAIL:
+            return chunks - 1
+        if offset > 0:
+            return chunk if chunk >= start else chunk - offset
+        return min(chunk - offset, chunks - 1)
+
     def push(turn):
         own_due = turn + OFF if EARLY <= turn + OFF < chunks else None
 
@@ -388,14 +391,12 @@
                 passed(turn, first_one)
             if own_due is not None:
                 own(own_due, first_one)
-            rest = [(c, True) for c in range(EARLY, chunks) if c >= SPLIT and c == turn + SHIFT]
-            if own_due is not None and own_due < SPLIT:
-                rest.append((own_due, True))
-            for c in range(DIRECT, chunks) if quarter else ():
-                if min(c + LEAD * (c >= LATE), chunks - 1) == turn:
-                    rest.append((c, False))
-            for c, mine in rest:
-                (own if mine else passed)(c, the_rest)
+            rest = [(c, 0) for c in range(EARLY, chunks) if later(c, SPLIT, OFF) == turn]
+            if quarter:
+                rest += [(c, 1) for c in range(DIRECT, chunks) if later(c, DIRECT, -LEAD) == turn]
+            rest.sort()
+            for c, relayed in rest:
+                (passed if relayed else own)(c, the_rest)
 
     pushed = 0
     for turn in range(chunks + LAG):

time: 32.6 us -> 32.2 us (0.988)
  Pallas kernels: 32.4 us -> 32 us
    pallas_call x1, Pallas kernels: 31.4 us -> 31 us  [body(): pl.pallas_call(functools.partial(kernel, n_ya, n_zb, bounds), out_shape=o...]
where the time goes in v4:
time: 32.2 us; the launch traced here: 32 us
  Pallas kernels  32 us (99%)
    pallas_call x1, Pallas kernels, body(): pl.pallas_call(functools.partial(kernel, n_ya, n_zb, bounds), out_shape=o...  31 us
    pallas_call x1, Pallas kernels, body(): pl.pallas_call(finish, out_shape=jax.ShapeDtypeStruct((kl, jl, nz), jnp.f...  1.01 us

profile of v4, /device:TPU:4, one launch (start us, length us, event | category | flops | bytes accessed | tf_op | source)
XLA Modules:
  0.0 32.0 jit_solution(11469606117037302733)
XLA Ops:
  0.0 31.0 %shard_map.73 = (f32[16,32,512]{2,1,0:T(8,128)S(1)}, f32[4,1,32,128]{3,2,1,0:T(8,128)S(1)}, f32[1,32,512]{2,1,0:T(8,128)S(1)}, bf16[2,512,512]{2,1,0:T(8,128)(2,1)S(1)}) custom-call(f32[128,16,128]{2,1,0:T(8,128)} %source.1, bf16[128,384]{1,0:T(8,128)(2,1)} %constant.4.clone.table_x.table_y, bf16[128,384]{1,0:T(8,128)(2,1)} %constant.4.clone.table_x.table_y, ...), custom_call_target="tpu_custom_call" | custom-call | tf_op jit(solution)/shard_map/pallas_call | solution.py:462
  31.0 1.0 %shard_map.74 = f32[16,32,512]{2,1,0:T(8,128)} custom-call(f32[16,32,512]{2,1,0:T(8,128)S(1)} %get-tuple-element.9.done, f32[4,1,32,128]{3,2,1,0:T(8,128)S(1)} %get-tuple-element.10.last, f32[1,32,512]{2,1,0:T(8,128)S(1)} %get-tuple-element.11.scale, bf16[2,512,512]{2,1,0:T(8,128)(2,1)S(1)} %get-tuple-element.12.table), custom_call_target="tpu_custom_call" | custom-call | tf_op jit(solution)/shard_map/pallas_call | solution.py:495
